TPU v7x, 32 devices: a whole 2x2x4 slice. The times are simulated.
32 devices in a mesh: seq: 2 (over core), mp: 4 (over y, x), batch: 4 (over z).
Axes of the slice: x: 2, y: 2, z: 4, core: 2. Of those that a mesh axis runs over, the one named last changes fastest.
Arguments:
- queries: bfloat16 [4, 8, 4096], P('batch', 'seq', 'mp'), may hold values from -6 to 6
- keys: bfloat16 [4, 512, 1024], P('batch', 'seq', 'mp'), may hold values from -6 to 6
- values: bfloat16 [4, 512, 1024], P('batch', 'seq', 'mp'), may hold values from -6 to 6
- key_position: float32 [32, 128], replicated, may hold values from -4 to 4
- compress_keys: bfloat16 [4096, 128], replicated, may hold values from -0.2 to 0.2
- compress_values: bfloat16 [4096, 128], replicated, may hold values from -0.09375 to 0.09375
- out_proj: bfloat16 [4096, 4096], P('mp', 'seq'), may hold values from -0.09375 to 0.09375
- residual: bfloat16 [4, 8, 4096], P(None, None, 'seq'), may hold values from -6 to 6
- norm_gain: float32 [4096], replicated, may hold values from 0.25 to 1.75
- lm_head: bfloat16 [8192, 4096], P(('seq', 'mp', 'batch')), may hold values from -0.4 to 0.4
- targets: int32 [4, 8], replicated, may hold values from 0 to 8191
- lengths: int32 [4], replicated, may hold values from 128 to 512
Outputs:
- token_logprob: float32 [4, 8], P('batch', 'seq')
- rollout_score: float32 [4], P('batch')
All inputs are finite; a program needn't handle non-finite values.
Results may differ from a plain program's by a relative error of at most 0.0005.
The roundings to bfloat16 on the way count: a program that leaves them out, or rounds other values in their place, can miss the bound.
Values may be sent and summed in bfloat16 or wider, within the bound.
No kernel may reach another device: no remote copies, remote signals or barrier semaphores. Data moves between devices by JAX's collectives and lax.ppermute only.
A program may use at most 64 MiB of HBM per device.

v0:
```python
import math
import jax
import jax.numpy as jnp
from jax import lax
from jax.sharding import PartitionSpec as P

HEAD_DIM = 128
BLOCK = 32
STRIDE = 16


def from_behind(block, axis, distance):
    devices = range(lax.axis_size(axis))
    route = [(i - distance, i) for i in devices if i - distance in devices]
    return lax.ppermute(block, axis, route)


def compress_rows(rows, following, position, weight):
    extended = jnp.concatenate([rows, following], 0)
    count = rows.shape[0] // STRIDE
    heads = rows.shape[1] // HEAD_DIM
    shaped = extended.reshape(count + 1, STRIDE, heads, HEAD_DIM)
    blocks = jnp.concatenate([shaped[:-1], shaped[1:]], 1)
    blocks = (blocks.astype(jnp.float32) + position[None, :, None, :]).astype(jnp.bfloat16)
    mapped = jnp.einsum(
        "bjhd,jde->bhe",
        blocks,
        weight.reshape(BLOCK, HEAD_DIM, HEAD_DIM),
        preferred_element_type=jnp.float32,
    )
    return mapped.astype(jnp.bfloat16).reshape(count, heads * HEAD_DIM)


def normalize(hidden, gain):
    widened = hidden.astype(jnp.float32)
    meansq = jnp.mean(widened * widened, -1, keepdims=True)
    return (widened * lax.rsqrt(meansq + 1e-05) * gain).astype(jnp.bfloat16)


def vocab_logits(normed, rows):
    return lax.dot_general(
        normed, rows, (((1,), (1,)), ((), ())), preferred_element_type=jnp.float32
    )


def picked_logit(logits, offset, wanted):
    columns = offset + jnp.arange(logits.shape[1], dtype=jnp.int32)
    hits = columns[None, :] == wanted[:, None]
    return jnp.sum(jnp.where(hits, logits, 0.0), 1)


def body(
    queries,
    keys,
    values,
    key_position,
    compress_keys,
    compress_values,
    out_proj,
    residual,
    norm_gain,
    lm_head,
    targets,
    lengths,
):
    seq_count = lax.axis_size("seq")
    seq_pos = lax.axis_index("seq")
    batch_count = lax.axis_size("batch")
    batch_pos = lax.axis_index("batch")
    qcount = queries.shape[1]
    skip = keys.shape[1] // qcount
    scored = targets.shape[1]
    following = from_behind((keys[0, :STRIDE], values[0, :STRIDE]), "seq", -1)
    comp_keys = compress_rows(keys[0], following[0], key_position, compress_keys)
    comp_values = compress_rows(values[0], following[1], key_position, compress_values)
    every = lax.all_gather(jnp.stack([comp_keys, comp_values], 0), "seq", axis=1, tiled=True)
    heads = keys.shape[2] // HEAD_DIM
    blocks = every.shape[1]
    all_keys = every[0].reshape(blocks, heads, HEAD_DIM)
    all_values = every[1].reshape(blocks, heads, HEAD_DIM)
    group = queries.shape[2] // HEAD_DIM // heads
    query = queries[0].reshape(qcount, heads, group, HEAD_DIM)
    scores = jnp.einsum("qhgd,bhd->qhgb", query, all_keys, preferred_element_type=jnp.float32) * (
        1.0 / math.sqrt(HEAD_DIM)
    )
    index = seq_pos * qcount + jnp.arange(qcount, dtype=jnp.int32)
    limit = index * skip // STRIDE
    visible = (jnp.arange(blocks, dtype=jnp.int32)[None, :] <= limit[:, None])[:, None, None, :]
    scores = jnp.where(visible, scores, -1e30)
    peak = jnp.max(scores, -1, keepdims=True)
    weights = jnp.where(visible, jnp.exp(scores - peak), 0.0)
    probs = (weights / jnp.sum(weights, -1, keepdims=True)).astype(jnp.bfloat16)
    attended = jnp.einsum("qhgb,bhd->qhgd", probs, all_values, preferred_element_type=jnp.float32)
    attended = attended.astype(jnp.bfloat16).reshape(qcount, heads * group * HEAD_DIM)
    spots = jnp.arange(scored, dtype=jnp.int32) * skip + BLOCK - 1
    valid = (spots[None, :] < lengths[:, None]).astype(jnp.float32)
    count = jnp.sum(valid)
    width = out_proj.shape[1]
    rows_all = lax.all_gather(attended, ("seq", "batch"), axis=0, tiled=True)
    part = jnp.dot(rows_all, out_proj, preferred_element_type=jnp.float32)
    summed = lax.psum(part, "mp")
    local_res = (
        residual.reshape(batch_count, seq_count, qcount, width)
        .transpose(1, 0, 2, 3)
        .reshape(-1, width)
    )
    hidden = (local_res.astype(jnp.float32) + summed).astype(jnp.bfloat16)
    whole = lax.all_gather(hidden, "seq", axis=1, tiled=True)
    normed = normalize(whole, norm_gain)
    logits = vocab_logits(normed, lm_head)
    wanted = targets.reshape(batch_count, seq_count, qcount).transpose(1, 0, 2).reshape(-1)
    offset = lax.axis_index(("seq", "mp", "batch")) * lm_head.shape[0]
    picked = picked_logit(logits, offset, wanted)
    local_top = jnp.max(logits, 1)
    top = lax.pmax(local_top, ("seq", "mp", "batch"))
    local_sum = jnp.sum(jnp.exp(logits - top[:, None]), 1)
    total, target_logit = lax.psum((local_sum, picked), ("seq", "mp", "batch"))
    logprob = target_logit - (top + jnp.log(total))
    cube = logprob.reshape(seq_count, batch_count, qcount)
    token_logprob = cube[seq_pos, batch_pos][None, :]
    by_rollout = cube.transpose(1, 0, 2).reshape(batch_count, scored)
    sums = jnp.sum(valid * by_rollout, 1) / count
    rollout_score = sums[batch_pos][None]
    return (token_logprob, rollout_score)


def solution(mesh):
    in_specs = (
        P("batch", "seq", "mp"),
        P("batch", "seq", "mp"),
        P("batch", "seq", "mp"),
        P(),
        P(),
        P(),
        P("mp", "seq"),
        P(None, None, "seq"),
        P(),
        P(("seq", "mp", "batch"), None),
        P(),
        P(),
    )
    out_specs = (P("batch", "seq"), P("batch"))
    return jax.shard_map(body, mesh=mesh, in_specs=in_specs, out_specs=out_specs, check_vma=False)
```

profile of v0, /device:TPU:0, one launch (start us, length us, event | category | flops | bytes accessed | tf_op | source)
XLA Modules:
  0.0 194.4 jit_solution(1485913314387452292)
XLA Ops:
  7.2 0.0 copy-start
  7.2 0.0 all-reduce.3.cloned.1.call-start
  7.2 0.9 slice_bitcast_fusion.1
  8.1 1.4 collective-permute-start
  9.5 1.3 slice_bitcast_fusion
  10.8 1.3 collective-permute-start.1
  12.1 0.6 iota_compare_fusion
  12.7 0.6 multiply_add_fusion
  13.3 0.9 slice.32
  14.3 0.9 slice.36
  15.2 0.7 copy.47
  15.9 0.1 copy.50
  16.0 1.3 reshape_squeeze.11
  17.3 0.9 pad_maximum_fusion.1
  18.2 0.1 copy.48
  18.3 1.6 fusion.6
  19.9 0.9 pad_maximum_fusion
  20.9 0.0 copy-start.2
  20.9 0.1 copy.51
  21.0 0.0 copy-start.4
  21.0 0.0 copy-start.6
  21.0 1.0 fusion.7
  22.0 0.0 copy-start.3
  22.1 2.6 %all_gather.9 = bf16[2,32,256]{2,1,0:T(8,128)(2,1)S(1)} all-gather(bf16[2,16,256]{2,1,0:T(8,128)(2,1)S(1)} %pad_maximum_fusion.2), channel_id=1, replica_groups=mesh['seq'=2,'mp'=4,'batch'=4] {'seq'}, dimensions={1}, use_global_device_ids=true | all-gather | bytes 49152 | tf_op jit(solution)/shard_map/all_gather | solution.py:76
  24.7 0.8 fusion.5
  25.5 0.8 fusion.32
  26.4 0.9 fusion.8
  27.3 25.7 %all-gather = bf16[8,4,1024]{2,1,0:T(4,128)(2,1)S(1)} all-gather(bf16[1,4,1024]{2,1,0:T(4,128)(2,1)S(1)} %reshape.113), channel_id=1, replica_groups=mesh['seq'=2,'mp'=4,'batch'=4] {'seq','batch'}, dimensions={0}, use_global_device_ids=true | all-gather | bytes 73728 | tf_op jit(solution)/shard_map/all_gather | solution.py:99
  53.0 3.7 %fusion.34 = f32[32,2048]{1,0:T(8,128)} fusion(bf16[32,1024]{1,0:T(8,128)(2,1)S(1)} %reshape.114, bf16[1024,2048]{1,0:T(8,128)(2,1)} %param.18), kind=kOutput, calls=%fused_computation.65 | convolution fusion | flops 134217728 | bytes 4521984 | tf_op jit(solution)/shard_map/dot_general | solution.py:100
  56.7 0.0 all-reduce.3.cloned.1.call-update
  56.8 0.1 reshape.112
  56.9 0.1 reshape.111
  57.0 0.1 reshape.106
  57.1 0.1 eq.16
  57.2 0.7 convert_reduce_fusion
  57.9 43.1 %all-reduce.3.cloned.1.call-done = f32[32,2048]{1,0:T(8,128)} async-done(((f32[32,2048]{1,0:T(8,128)}), f32[32,2048]{1,0:T(8,128)}) %all-reduce.3.cloned.1.call-update) | async-done | bytes 262160 | tf_op jit(solution)/shard_map/psum | solution.py:101
  101.0 1.0 add_convert_fusion.4
  102.0 2.0 %all_gather.11 = bf16[32,4096]{1,0:T(8,128)(2,1)S(1)} all-gather(bf16[32,2048]{1,0:T(8,128)(2,1)S(1)} %add_convert_fusion.4), channel_id=1, replica_groups=mesh['seq'=2,'mp'=4,'batch'=4] {'seq'}, dimensions={1}, use_global_device_ids=true | all-gather | bytes 393216 | tf_op jit(solution)/shard_map/all_gather | solution.py:108
  104.0 0.2 fusion.9
  104.2 0.8 fusion.33
  105.0 39.3 %pmax.7 = f32[32]{0:T(128)S(1)} all-reduce(f32[32]{0:T(128)S(1)} %get-tuple-element.8), channel_id=1, replica_groups=mesh['seq'=2,'mp'=4,'batch'=4] {'seq','mp','batch'}, use_global_device_ids=true, to_apply=%region_7.8 | all-reduce | flops 32 | bytes 256 | tf_op jit(solution)/shard_map/pmax | solution.py:115
  144.3 0.2 exponential_reduce_fusion
  144.5 41.0 %all-reduce = (f32[32]{0:T(128)S(1)}, f32[32]{0:T(128)S(1)}) all-reduce(f32[32]{0:T(128)S(1)} %get-tuple-element.3, f32[32]{0:T(128)S(1)} %get-tuple-element.2), channel_id=1, replica_groups=mesh['seq'=2,'mp'=4,'batch'=4] {'seq','mp','batch'}, use_global_device_ids=true, to_apply=%region_5.6 | all-reduce | flops 64 | bytes 512 | tf_op jit(solution)/shard_map/psum | solution.py:117
  185.5 0.1 reshape.110
  185.6 0.2 fusion.28
  185.8 0.7 broadcast_divide_fusion
  186.4 0.6 dynamic_slice.7
  187.0 0.5 dynamic-slice_bitcast_fusion
  (31 shorter events, 0.3 us)
Async XLA Ops:
  7.2 97.0 %copy-start = (bf16[256,4096]{1,0:T(8,128)(2,1)S(1)}, bf16[256,4096]{1,0:T(8,128)(2,1)}, u32[]{:S(2)}) copy-start(bf16[256,4096]{1,0:T(8,128)(2,1)} %param.21) | copy-start | bytes 6291460
  7.2 13.8 %copy-start.1 = (bf16[4096,128]{1,0:T(8,128)(2,1)S(1)}, bf16[4096,128]{1,0:T(8,128)(2,1)}, u32[]{:S(2)}) copy-start(bf16[4096,128]{1,0:T(8,128)(2,1)} %param.17) | copy-start | bytes 3145732
  7.2 93.8 %all-reduce.3.cloned.1.call-start = ((), (), s32[]{:S(2)}) async-start(), calls=%async_computation | async-start | bytes 524288 | tf_op jit(solution)/shard_map/psum | solution.py:101
  8.1 9.1 %collective-permute-start = (bf16[16,256]{1,0:T(8,128)(2,1)S(1)}, bf16[16,256]{1,0:T(8,128)(2,1)S(1)}, u32[]{:S(2)}, u32[]{:S(2)}) collective-permute-start(bf16[16,256]{1,0:T(8,128)(2,1)S(1)} %slice_bitcast_fusion.1), channel_id=1, source_target_pairs={{16,0},{17,1},{18,2},{19,3},{20,4},{21,5},{22,6},{23,7},{24,8},{25... | collective-permute-start | bytes 24584 | tf_op jit(solution)/shard_map/ppermute | solution.py:15
  10.8 9.1 %collective-permute-start.1 = (bf16[16,256]{1,0:T(8,128)(2,1)}, bf16[16,256]{1,0:T(8,128)(2,1)S(1)}, u32[]{:S(2)}, u32[]{:S(2)}) collective-permute-start(bf16[16,256]{1,0:T(8,128)(2,1)} %slice_bitcast_fusion), channel_id=1, source_target_pairs={{16,0},{17,1},{18,2},{19,3},{20,4},{21,5},{22,6},{23,7},{24,8},{25... | collective-permute-start | bytes 24584 | tf_op jit(solution)/shard_map/ppermute | solution.py:15
  20.9 35.9 %copy-start.2 = (bf16[4,8,2048]{2,1,0:T(8,128)(2,1)S(1)}, bf16[4,8,2048]{2,1,0:T(8,128)(2,1)}, u32[]{:S(2)}) copy-start(bf16[4,8,2048]{2,1,0:T(8,128)(2,1)} %param.19) | copy-start | bytes 393220
  21.0 36.0 %copy-start.4 = (s32[4,8]{1,0:T(4,128)S(1)}, s32[4,8]{1,0:T(4,128)}, u32[]{:S(2)}) copy-start(s32[4,8]{1,0:T(4,128)} %param.22) | copy-start | bytes 388
  21.0 36.2 %copy-start.6 = (s32[4]{0:T(128)S(1)}, s32[4]{0:T(128)}, u32[]{:S(2)}) copy-start(s32[4]{0:T(128)} %param.23) | copy-start | bytes 52
  22.0 82.1 %copy-start.3 = (f32[4096]{0:T(1024)S(1)}, f32[4096]{0:T(1024)}, u32[]{:S(2)}) copy-start(f32[4096]{0:T(1024)} %param.20) | copy-start | bytes 49156
  53.0 132.6 %copy-start.5 = (s32[2,4]{1,0:T(2,128)S(1)}, s32[2,4]{1,0:T(2,128)}, u32[]{:S(2)}) copy-start(s32[2,4]{1,0:T(2,128)} %multiply_add_fusion) | copy-start | bytes 100
Sparse Core Ops, SparseCore 0:
  56.9 44.0 all-reduce.2
where the time goes:
time: 195 us; the launch traced here: 194 us
  blocking collectives  111 us (57%)
  waiting for transfers between devices  43.1 us (22%)
  between operations  14.3 us (7%)
  matrix products  8.86 us (5%)
  local copies, waits for them, and re-layouts  8.01 us (4%)
  other arithmetic  6.72 us (3%)
  starting transfers between devices  2.73 us (1%)
    psum x1, waiting for transfers between devices, body(): summed = lax.psum(part, 'mp')  43.1 us
    psum x1, blocking collectives, body(): total, target_logit = lax.psum((local_sum, picked), ('seq', 'mp', 'batch'))  41 us
    pmax x1, blocking collectives, body(): top = lax.pmax(local_top, ('seq', 'mp', 'batch'))  39.3 us
    all_gather x1, blocking collectives, body(): rows_all = lax.all_gather(attended, ('seq', 'batch'), axis=0, tiled=True)  25.7 us
  transfers between devices with their start and end apart: 3, of which 1 were waited for; matrix products, arithmetic and copies ran while one was open for 5% of the time, Pallas kernels for 0%

commit v1 on v0

--- a/solution.py
+++ b/solution.py
@@ -96,7 +96,15 @@
     valid = (spots[None, :] < lengths[:, None]).astype(jnp.float32)
     count = jnp.sum(valid)
     width = out_proj.shape[1]
-    rows_all = lax.all_gather(attended, ("seq", "batch"), axis=0, tiled=True)
+    ways, here = (lax.axis_size(("seq", "batch")), lax.axis_index(("seq", "batch")))
+    grown, reach = (attended, 1)
+    while reach < ways:
+        theirs = lax.ppermute(grown, ("seq", "batch"), [(d, d ^ reach) for d in range(ways)])
+        mine_first = jnp.concatenate([grown, theirs], axis=0)
+        theirs_first = jnp.concatenate([theirs, grown], axis=0)
+        grown = jnp.where(here & reach == 0, mine_first, theirs_first)
+        reach = 2 * reach
+    rows_all = grown
     part = jnp.dot(rows_all, out_proj, preferred_element_type=jnp.float32)
     summed = lax.psum(part, "mp")
     local_res = (

time: 195 us -> 180 us (0.923)
  blocking collectives: 111 us -> 84.9 us
  starting transfers between devices: 2.73 us -> 9.02 us
  waiting for transfers between devices: 43.1 us -> 48.3 us
    all_gather x1 -> x0, blocking collectives: 25.7 us -> none  [body(): rows_all = lax.all_gather(attended, ('seq', 'batch'), axis=0, tiled=True)]
    ppermute x0 -> x3, starting transfers between devices: none -> 6.29 us  [body(): lax.ppermute(grown, ('seq', 'batch'), [(d, d ^ reach) for d in range(ways)])]
    ppermute x0 -> x3, waiting for transfers between devices: none -> 4.53 us  [body(): lax.ppermute(grown, ('seq', 'batch'), [(d, d ^ reach) for d in range(ways)])]
  transfers between devices with their start and end apart: 3 -> 6, of which waited for: 1 -> 4; matrix products, arithmetic and copies ran while one was open for 5% -> 5% of each run, Pallas kernels for 0% -> 0%
where the time goes in v1:
time: 180 us
  blocking collectives  84.9 us (47%)
  waiting for transfers between devices  48.3 us (27%)
  between operations  14.3 us (8%)
  starting transfers between devices  9.02 us (5%)
  matrix products  8.86 us (5%)
  local copies, waits for them, and re-layouts  7.98 us (4%)
  other arithmetic  6.16 us (3%)
    psum x1, waiting for transfers between devices, body(): summed = lax.psum(part, 'mp')  43.8 us
    psum x1, blocking collectives, body(): total, target_logit = lax.psum((local_sum, picked), ('seq', 'mp', 'batch'))  41 us
    pmax x1, blocking collectives, body(): top = lax.pmax(local_top, ('seq', 'mp', 'batch'))  39.3 us
    ppermute x3, starting transfers between devices, body(): lax.ppermute(grown, ('seq', 'batch'), [(d, d ^ reach) for d in range(ways)])  6.29 us
    ppermute x3, waiting for transfers between devices, body(): lax.ppermute(grown, ('seq', 'batch'), [(d, d ^ reach) for d in range(ways)])  4.53 us
    dot_general x1, matrix products, body(): part = jnp.dot(rows_all, out_proj, preferred_element_type=jnp.float32)  3.72 us
  transfers between devices with their start and end apart: 6, of which 4 were waited for; matrix products, arithmetic and copies ran while one was open for 5% of the time, Pallas kernels for 0%

profile of v1, /device:TPU:0, one launch (start us, length us, event | category | flops | bytes accessed | tf_op | source)
XLA Modules:
  0.0 179.6 jit_solution(5402693705473911101)
XLA Ops:
  7.2 0.0 copy-start
  7.2 0.0 all-reduce.3.cloned.1.call-start
  7.2 0.9 slice_bitcast_fusion.1
  8.1 1.4 collective-permute-start
  9.5 1.3 slice_bitcast_fusion
  10.8 1.3 collective-permute-start.1
  12.1 0.6 iota_compare_fusion
  12.7 0.9 slice.32
  13.7 0.9 slice.36
  14.6 0.7 copy.35
  15.3 0.1 copy.38
  15.4 1.3 reshape_squeeze.11
  16.7 0.9 pad_maximum_fusion.1
  17.6 0.1 copy.36
  17.7 1.6 fusion.6
  19.3 0.9 pad_maximum_fusion
  20.3 0.1 copy.39
  20.4 1.0 fusion.7
  21.5 2.6 %all_gather.6 = bf16[2,32,256]{2,1,0:T(8,128)(2,1)S(1)} all-gather(bf16[2,16,256]{2,1,0:T(8,128)(2,1)S(1)} %pad_maximum_fusion.2), channel_id=1, replica_groups=mesh['seq'=2,'mp'=4,'batch'=4] {'seq'}, dimensions={1}, use_global_device_ids=true | all-gather | bytes 49152 | tf_op jit(solution)/shard_map/all_gather | solution.py:76
  24.1 0.8 fusion.5
  24.9 0.8 fusion.40
  25.8 0.9 fusion.8
  26.7 3.1 %collective-permute-start.2 = (bf16[4,1024]{1,0:T(4,128)(2,1)S(1)}, bf16[4,1024]{1,0:T(4,128)(2,1)S(1)}, u32[]{:S(2)}, u32[]{:S(2)}) collective-permute-start(bf16[4,1024]{1,0:T(4,128)(2,1)S(1)} %reshape.109), channel_id=1, source_target_pairs={{0,1},{1,0},{2,3},{3,2},{16,17},{17,16},{18,19},{19,18},{4,5},{5,4... | collective-permute-start | bytes 24584 | tf_op jit(solution)/shard_map/ppermute | solution.py:102
  29.8 1.6 collective-permute-done.2
  31.4 3.1 %collective-permute-start.3 = (bf16[8,1024]{1,0:T(8,128)(2,1)S(1)}, bf16[8,1024]{1,0:T(8,128)(2,1)S(1)}, u32[]{:S(2)}, u32[]{:S(2)}) collective-permute-start(bf16[8,1024]{1,0:T(8,128)(2,1)S(1)} %maximum_select_fusion.3), channel_id=1, source_target_pairs={{0,2},{1,3},{2,0},{3,1},{16,18},{17,19},{18,16},{19,17},{4,6},{5,7... | collective-permute-start | bytes 49160 | tf_op jit(solution)/shard_map/ppermute | solution.py:102
  34.5 1.7 collective-permute-done.3
  36.3 0.1 collective-permute-start.4
  36.4 1.2 collective-permute-done.4
  37.5 3.7 %fusion.24 = f32[32,2048]{1,0:T(8,128)} fusion(bf16[1024,2048]{1,0:T(8,128)(2,1)} %param.18, bf16[16,1024]{1,0:T(8,128)(2,1)S(1)} %collective-permute-done.4, bf16[16,1024]{1,0:T(8,128)(2,1)S(1)} %maximum_select_fusion.2, pred[]{:T(512)S(6)} %eq.28), kind=kOutput, calls=%fused_computation.36 | convolution fusion | flops 134512640 | bytes 4521985 | tf_op jit(solution)/shard_map/dot_general | solution.py:108
  41.2 0.0 all-reduce.3.cloned.1.call-update
  41.3 0.1 reshape.112
  41.4 0.1 reshape.111
  41.5 0.1 reshape.106
  41.6 0.1 eq.25
  41.7 0.7 convert_reduce_fusion
  42.4 43.8 %all-reduce.3.cloned.1.call-done = f32[32,2048]{1,0:T(8,128)} async-done(((f32[32,2048]{1,0:T(8,128)}), f32[32,2048]{1,0:T(8,128)}) %all-reduce.3.cloned.1.call-update) | async-done | bytes 262160 | tf_op jit(solution)/shard_map/psum | solution.py:109
  86.2 1.0 add_convert_fusion.4
  87.2 2.0 %all_gather.7 = bf16[32,4096]{1,0:T(8,128)(2,1)S(1)} all-gather(bf16[32,2048]{1,0:T(8,128)(2,1)S(1)} %add_convert_fusion.4), channel_id=1, replica_groups=mesh['seq'=2,'mp'=4,'batch'=4] {'seq'}, dimensions={1}, use_global_device_ids=true | all-gather | bytes 393216 | tf_op jit(solution)/shard_map/all_gather | solution.py:116
  89.1 0.2 fusion.9
  89.3 0.8 fusion.41
  90.2 39.3 %pmax.7 = f32[32]{0:T(128)S(1)} all-reduce(f32[32]{0:T(128)S(1)} %get-tuple-element.8), channel_id=1, replica_groups=mesh['seq'=2,'mp'=4,'batch'=4] {'seq','mp','batch'}, use_global_device_ids=true, to_apply=%region_7.8 | all-reduce | flops 32 | bytes 256 | tf_op jit(solution)/shard_map/pmax | solution.py:123
  129.5 0.2 exponential_reduce_fusion
  129.7 41.0 %all-reduce = (f32[32]{0:T(128)S(1)}, f32[32]{0:T(128)S(1)}) all-reduce(f32[32]{0:T(128)S(1)} %get-tuple-element.3, f32[32]{0:T(128)S(1)} %get-tuple-element.2), channel_id=1, replica_groups=mesh['seq'=2,'mp'=4,'batch'=4] {'seq','mp','batch'}, use_global_device_ids=true, to_apply=%region_5.6 | all-reduce | flops 64 | bytes 512 | tf_op jit(solution)/shard_map/psum | solution.py:125
  170.7 0.1 reshape.110
  170.8 0.2 fusion.35
  170.9 0.7 broadcast_divide_fusion
  171.6 0.6 dynamic_slice.7
  172.2 0.5 dynamic-slice_bitcast_fusion
  (35 shorter events, 0.3 us)
Async XLA Ops:
  7.2 82.2 %copy-start = (bf16[256,4096]{1,0:T(8,128)(2,1)S(1)}, bf16[256,4096]{1,0:T(8,128)(2,1)}, u32[]{:S(2)}) copy-start(bf16[256,4096]{1,0:T(8,128)(2,1)} %param.21) | copy-start | bytes 6291460
  7.2 13.2 %copy-start.1 = (bf16[4096,128]{1,0:T(8,128)(2,1)S(1)}, bf16[4096,128]{1,0:T(8,128)(2,1)}, u32[]{:S(2)}) copy-start(bf16[4096,128]{1,0:T(8,128)(2,1)} %param.17) | copy-start | bytes 3145732
  7.2 79.0 %all-reduce.3.cloned.1.call-start = ((), (), s32[]{:S(2)}) async-start(), calls=%async_computation | async-start | bytes 524288 | tf_op jit(solution)/shard_map/psum | solution.py:109
  8.1 8.5 %collective-permute-start = (bf16[16,256]{1,0:T(8,128)(2,1)S(1)}, bf16[16,256]{1,0:T(8,128)(2,1)S(1)}, u32[]{:S(2)}, u32[]{:S(2)}) collective-permute-start(bf16[16,256]{1,0:T(8,128)(2,1)S(1)} %slice_bitcast_fusion.1), channel_id=1, source_target_pairs={{16,0},{17,1},{18,2},{19,3},{20,4},{21,5},{22,6},{23,7},{24,8},{25... | collective-permute-start | bytes 24584 | tf_op jit(solution)/shard_map/ppermute | solution.py:15
  10.8 8.5 %collective-permute-start.1 = (bf16[16,256]{1,0:T(8,128)(2,1)}, bf16[16,256]{1,0:T(8,128)(2,1)S(1)}, u32[]{:S(2)}, u32[]{:S(2)}) collective-permute-start(bf16[16,256]{1,0:T(8,128)(2,1)} %slice_bitcast_fusion), channel_id=1, source_target_pairs={{16,0},{17,1},{18,2},{19,3},{20,4},{21,5},{22,6},{23,7},{24,8},{25... | collective-permute-start | bytes 24584 | tf_op jit(solution)/shard_map/ppermute | solution.py:15
  20.3 21.0 %copy-start.2 = (bf16[4,8,2048]{2,1,0:T(8,128)(2,1)S(1)}, bf16[4,8,2048]{2,1,0:T(8,128)(2,1)}, u32[]{:S(2)}) copy-start(bf16[4,8,2048]{2,1,0:T(8,128)(2,1)} %param.19) | copy-start | bytes 393220
  20.4 21.2 %copy-start.4 = (s32[4,8]{1,0:T(4,128)S(1)}, s32[4,8]{1,0:T(4,128)}, u32[]{:S(2)}) copy-start(s32[4,8]{1,0:T(4,128)} %param.22) | copy-start | bytes 388
  20.4 21.3 %copy-start.5 = (s32[4]{0:T(128)S(1)}, s32[4]{0:T(128)}, u32[]{:S(2)}) copy-start(s32[4]{0:T(128)} %param.23) | copy-start | bytes 52
  21.4 67.9 %copy-start.3 = (f32[4096]{0:T(1024)S(1)}, f32[4096]{0:T(1024)}, u32[]{:S(2)}) copy-start(f32[4096]{0:T(1024)} %param.20) | copy-start | bytes 49156
  26.7 4.7 %collective-permute-start.2 = (bf16[4,1024]{1,0:T(4,128)(2,1)S(1)}, bf16[4,1024]{1,0:T(4,128)(2,1)S(1)}, u32[]{:S(2)}, u32[]{:S(2)}) collective-permute-start(bf16[4,1024]{1,0:T(4,128)(2,1)S(1)} %reshape.109), channel_id=1, source_target_pairs={{0,1},{1,0},{2,3},{3,2},{16,17},{17,16},{18,19},{19,18},{4,5},{5,4... | collective-permute-start | bytes 24584 | tf_op jit(solution)/shard_map/ppermute | solution.py:102
  31.4 4.8 %collective-permute-start.3 = (bf16[8,1024]{1,0:T(8,128)(2,1)S(1)}, bf16[8,1024]{1,0:T(8,128)(2,1)S(1)}, u32[]{:S(2)}, u32[]{:S(2)}) collective-permute-start(bf16[8,1024]{1,0:T(8,128)(2,1)S(1)} %maximum_select_fusion.3), channel_id=1, source_target_pairs={{0,2},{1,3},{2,0},{3,1},{16,18},{17,19},{18,16},{19,17},{4,6},{5,7... | collective-permute-start | bytes 49160 | tf_op jit(solution)/shard_map/ppermute | solution.py:102
  36.3 1.3 collective-permute-start.4
Sparse Core Ops, SparseCore 0:
  41.4 44.7 all-reduce.2
